TPU v7x, 32 devices: a whole 2x2x4 slice. The times are simulated.
32 devices in a mesh: gx: 2 (over x), gy: 4 (over y, core), gz: 4 (over z).
Axes of the slice: x: 2, y: 2, z: 4, core: 2. Of those that a mesh axis runs over, the one named last changes fastest.
Arguments:
- right_side: float32 [4, 5, 2, 32, 512], P(None, None, 'gx', 'gy', 'gz'), may hold values from -6 to 6
- jacobian: bfloat16 [27, 5, 5, 2, 32, 512], P(None, None, None, 'gx', 'gy', 'gz'), may hold values from -0.14 to 12.14, as said below
Outputs:
- solution: float32 [4, 5, 2, 32, 512], P(None, None, 'gx', 'gy', 'gz')
- residual: float32 [4, 5, 2, 32, 512], P(None, None, 'gx', 'gy', 'gz')
Inputs may be any that keep to these rules, and one draw needn't show every extreme that they name: `jacobian`: blocks of offsets other than 13 and the off-diagonal entries of block 13 lie within -0.14 to 0.14; the diagonal entries of block 13 exceed 5.8 in every cell.
All inputs are finite; a program needn't handle non-finite values.
Results may differ from a plain program's by a relative error of at most 0.0003.
Values sent between devices are 32-bit elements.
No kernel may reach another device: no remote copies, remote signals or barrier semaphores. Data moves between devices by JAX's collectives and lax.ppermute only.
A program may use at most 64 MiB of HBM per device.

v0:
```python
import jax
import jax.numpy as jnp
from jax import lax
from jax.sharding import PartitionSpec as P

ITERS = 3


def extended(cells, sides, width):
    for axis, dim in sides:
        count = lax.axis_size(axis)
        head = lax.slice_in_dim(cells, 0, width, axis=dim)
        tail = lax.slice_in_dim(cells, cells.shape[dim] - width, cells.shape[dim], axis=dim)
        cells = jnp.concatenate(
            [
                lax.ppermute(tail, axis, [(i, (i + 1) % count) for i in range(count)]),
                cells,
                lax.ppermute(head, axis, [((i + 1) % count, i) for i in range(count)]),
            ],
            axis=dim,
        )
    return cells


def dot_high(left, right):
    return jnp.dot(left, right, precision=lax.Precision.HIGHEST, preferred_element_type=jnp.float32)


def lower_solve(factor, target):
    solved = []
    for row_pos in range(factor.shape[0]):
        accum = target[row_pos]
        for prior in range(row_pos):
            accum = accum - factor[row_pos, prior] * solved[prior]
        solved.append(accum / factor[row_pos, row_pos])
    return jnp.stack(solved)


def upper_solve(factor, target):
    size_all = factor.shape[0]
    solved = [None] * size_all
    for row_pos in range(size_all - 1, -1, -1):
        accum = target[row_pos]
        for later in range(row_pos + 1, size_all):
            accum = accum - factor[later, row_pos] * solved[later]
        solved[row_pos] = accum / factor[row_pos, row_pos]
    return jnp.stack(solved)


def extend(field):
    padded = extended(field, (("gx", 2), ("gy", 3), ("gz", 4)), 1)
    position = lax.axis_index("gz")
    bottom = jnp.where(position == 0, 0.0, 1.0).astype(jnp.float32)
    topmost = jnp.where(position == lax.axis_size("gz") - 1, 0.0, 1.0).astype(jnp.float32)
    inside = jnp.ones((padded.shape[4] - 2,), jnp.float32)
    scaling = jnp.concatenate([bottom[None], inside, topmost[None]])
    return padded * scaling


def apply_operator(jacobian, padded):
    extent_x = padded.shape[2] - 2
    extent_y = padded.shape[3] - 2
    extent_z = padded.shape[4] - 2
    total = jnp.zeros((padded.shape[0], padded.shape[1], extent_x, extent_y, extent_z), jnp.float32)
    for stencil_pos in range(27):
        start_x = stencil_pos // 9
        start_y = stencil_pos // 3 % 3
        start_z = stencil_pos % 3
        piece = padded[
            :,
            :,
            start_x : start_x + extent_x,
            start_y : start_y + extent_y,
            start_z : start_z + extent_z,
        ]
        block = jacobian[stencil_pos].astype(jnp.float32)
        for source_comp in range(block.shape[1]):
            total = total + block[None, :, source_comp] * piece[:, source_comp][:, None]
    return total


def shards(right_side, jacobian):
    field_shape = right_side.shape
    rhs_count = field_shape[0]
    flat_rhs = right_side.reshape(rhs_count, -1)
    start_matrix = lax.psum(dot_high(flat_rhs, flat_rhs.T), ("gx", "gy", "gz"))
    start_factor = jnp.linalg.cholesky(start_matrix)
    basis = [lower_solve(start_factor, flat_rhs)]
    hessen_rows = []
    products = []
    for iteration in range(ITERS):
        workspace = apply_operator(jacobian, extend(basis[-1].reshape(field_shape))).reshape(
            rhs_count, -1
        )
        products.append(workspace)
        stacked = jnp.concatenate(basis, axis=0)
        coefficients, raw_gram = lax.psum(
            (dot_high(stacked, workspace.T), dot_high(workspace, workspace.T)), ("gx", "gy", "gz")
        )
        workspace = workspace - dot_high(coefficients.T, stacked)
        gram_matrix = raw_gram - dot_high(coefficients.T, coefficients)
        factor = jnp.linalg.cholesky(gram_matrix)
        basis.append(lower_solve(factor, workspace))
        filler = jnp.zeros((rhs_count, rhs_count * (ITERS - iteration - 1)), jnp.float32)
        hessen_rows.append(jnp.concatenate([coefficients.T, factor, filler], axis=1))
    hessen = jnp.concatenate(hessen_rows, axis=0)
    target = jnp.concatenate(
        [start_factor, jnp.zeros((rhs_count, rhs_count * ITERS), jnp.float32)], axis=1
    )
    normal_factor = jnp.linalg.cholesky(dot_high(hessen, hessen.T))
    middle = lower_solve(normal_factor, dot_high(hessen, target.T))
    weights = upper_solve(normal_factor, middle)
    solution = dot_high(weights.T, jnp.concatenate(basis[:-1], axis=0))
    solution_field = solution.reshape(field_shape)
    residual = right_side - apply_operator(jacobian, extend(solution_field))
    return (solution_field, residual)


def solution(mesh):
    in_specs = (P(None, None, "gx", "gy", "gz"), P(None, None, None, "gx", "gy", "gz"))
    out_specs = (P(None, None, "gx", "gy", "gz"), P(None, None, "gx", "gy", "gz"))
    return jax.shard_map(shards, mesh=mesh, in_specs=in_specs, out_specs=out_specs, check_vma=False)
```

profile of v0, /device:TPU:0, one launch (start us, length us, event | category | flops | bytes accessed | tf_op | source)
XLA Modules:
  0.0 496.2 jit_solution(8846187615325379422)
XLA Ops:
  2.1 41.9 %psum.49 = f32[4,4]{0,1:T(4,128)S(1)} all-reduce(f32[4,4]{0,1:T(4,128)S(1)} %convolution_bitcast_fusion.4), channel_id=1, replica_groups=mesh['gx'=2,'gy'=4,'gz'=4] {'gx','gy','gz'}, use_global_device_ids=true, to_apply=%region_0.0 | all-reduce | flops 16 | bytes 128 | tf_op jit(solution)/shard_map/psum | solution.py:86
  46.6 4.5 subtract_divide_fusion.1
  51.0 5.3 %subtract_divide_fusion = (f32[1,5,1,8,128]{4,3,2,1,0:T(8,128)S(1)}, f32[1,5,1,8,128]{4,3,2,1,0:T(8,128)S(1)}, f32[1,5,1,8,128]{4,3,2,1,0:T(8,128)S(1)}, f32[1,5,1,8,128]{4,3,2,1,0:T(8,128)S(1)}) fusion(f32[1,5,1,8,128]{4,3,2,1,0:T(8,128)S(1)} %get-tuple-element.39, f32[1,5,1,8,128]{4,3,2,1,0:T(8,128)S(1)} %get-tuple-element.40, f32[]{:T(128)} %bitcast.16, ...), kind=kLoop, calls=%fused_computation.244 | loop fusion | flops 61440 | bytes 184348 | tf_op jit(solution)/shard_map/div | solution.py:35
  60.2 5.8 %subtract_divide_fusion.3 = (f32[1,5120]{1,0:T(1,128)S(1)}, f32[1,5120]{1,0:T(1,128)S(1)}, f32[1,5120]{1,0:T(1,128)S(1)}) fusion(f32[1,5120]{1,0:T(1,128)S(1)} %bitcast.1697, f32[1,5120]{1,0:T(1,128)S(1)} %bitcast.1646, f32[]{:T(128)} %bitcast.16, f32[]{:T(128)} %bitcast.15, f32[]{:T(128)} %bitcast.14, f32[]{:T(128)} %bitcast.13, f32[]{:T(128)} %bitcast.11, ...), kind=kLoop, calls=%fused_computation.248 | loop fusion | flops 76800 | bytes 143396 | tf_op jit(solution)/shard_map/div | solution.py:35
  72.6 11.6 %collective-permute-done.5 = f32[4,5,3,10,1]{4,3,2,1,0:T(8,128)S(1)} collective-permute-done((f32[4,5,3,10,1]{4,3,2,1,0:T(8,128)S(1)}, f32[4,5,3,10,1]{4,3,2,1,0:T(8,128)S(1)}, u32[]{:S(2)}, u32[]{:S(2)}) %collective-permute-start.5) | collective-permute-done | bytes 2432 | tf_op jit(solution)/shard_map/ppermute | solution.py:18
  84.2 11.7 %collective-permute-done.4 = f32[4,5,3,10,1]{4,3,2,1,0:T(8,128)S(1)} collective-permute-done((f32[4,5,3,10,1]{4,3,2,1,0:T(8,128)S(1)}, f32[4,5,3,10,1]{4,3,2,1,0:T(8,128)S(1)}, u32[]{:S(2)}, u32[]{:S(2)}) %collective-permute-start.4) | collective-permute-done | bytes 2432 | tf_op jit(solution)/shard_map/ppermute | solution.py:16
  100.5 38.5 %all-reduce.3 = (f32[4,4]{1,0:T(4,128)S(1)}, f32[4,4]{0,1:T(4,128)S(1)}) all-reduce(f32[4,4]{1,0:T(4,128)S(1)} %fusion.5, f32[4,4]{0,1:T(4,128)S(1)} %convolution_bitcast_fusion.3), channel_id=1, replica_groups=mesh['gx'=2,'gy'=4,'gz'=4] {'gx','gy','gz'}, use_global_device_ids=true, to_apply=%region_3.5 | all-reduce | flops 32 | bytes 256 | tf_op jit(solution)/shard_map/psum | solution.py:97
  142.0 6.5 %fusion.23 = (f32[1,5120]{1,0:T(1,128)S(1)}, f32[1,5120]{1,0:T(1,128)S(1)}, f32[1,5120]{1,0:T(1,128)S(1)}, f32[1,5120]{1,0:T(1,128)S(1)}) fusion(f32[4,5120]{1,0:T(4,128)S(1)} %convolution_subtract_fusion.1, f32[]{:T(128)} %bitcast.355, f32[]{:T(128)} %bitcast.354, f32[]{:T(128)} %bitcast.353, f32[]{:T(128)} %bitcast.352, f32[]{:T(128)} %bitcast.351, ...), kind=kLoop, calls=%fused_computation.254 | loop fusion | flops 81920 | bytes 163880 | tf_op jit(solution)/shard_map/div | solution.py:35
  162.2 11.6 %collective-permute-done.11 = f32[4,5,3,10,1]{4,3,2,1,0:T(8,128)} collective-permute-done((f32[4,5,3,10,1]{4,3,2,1,0:T(8,128)}, f32[4,5,3,10,1]{4,3,2,1,0:T(8,128)}, u32[]{:S(2)}, u32[]{:S(2)}) %collective-permute-start.11) | collective-permute-done | bytes 2432 | tf_op jit(solution)/shard_map/ppermute | solution.py:18
  173.8 10.6 %collective-permute-done.10 = f32[4,5,3,10,1]{4,3,2,1,0:T(8,128)} collective-permute-done((f32[4,5,3,10,1]{4,3,2,1,0:T(8,128)}, f32[4,5,3,10,1]{4,3,2,1,0:T(8,128)}, u32[]{:S(2)}, u32[]{:S(2)}) %collective-permute-start.10) | collective-permute-done | bytes 2432 | tf_op jit(solution)/shard_map/ppermute | solution.py:16
  190.2 38.3 %all-reduce.2 = (f32[8,4]{0,1:T(4,128)S(1)}, f32[4,4]{0,1:T(4,128)S(1)}) all-reduce(f32[8,4]{0,1:T(4,128)S(1)} %fusion.3, f32[4,4]{0,1:T(4,128)S(1)} %convolution_bitcast_fusion.2), channel_id=1, replica_groups=mesh['gx'=2,'gy'=4,'gz'=4] {'gx','gy','gz'}, use_global_device_ids=true, to_apply=%region_5.7 | all-reduce | flops 48 | bytes 384 | tf_op jit(solution)/shard_map/psum | solution.py:97
  231.4 6.5 %fusion.24 = (f32[1,5120]{1,0:T(1,128)S(1)}, f32[1,5120]{1,0:T(1,128)S(1)}, f32[1,5120]{1,0:T(1,128)S(1)}, f32[1,5120]{1,0:T(1,128)S(1)}) fusion(f32[4,5120]{1,0:T(4,128)S(1)} %convolution_subtract_fusion, f32[]{:T(128)} %bitcast.511, f32[]{:T(128)} %bitcast.510, f32[]{:T(128)} %bitcast.509, f32[]{:T(128)} %bitcast.508, f32[]{:T(128)} %bitcast.507, ...), kind=kLoop, calls=%fused_computation.255 | loop fusion | flops 81920 | bytes 163880 | tf_op jit(solution)/shard_map/div | solution.py:35
  240.4 2.7 collective-permute-done.13
  252.1 11.5 %collective-permute-done.17 = f32[4,5,3,10,1]{4,3,2,1,0:T(8,128)} collective-permute-done((f32[4,5,3,10,1]{4,3,2,1,0:T(8,128)}, f32[4,5,3,10,1]{4,3,2,1,0:T(8,128)}, u32[]{:S(2)}, u32[]{:S(2)}) %collective-permute-start.17) | collective-permute-done | bytes 2432 | tf_op jit(solution)/shard_map/ppermute | solution.py:18
  263.6 10.3 %collective-permute-done.16 = f32[4,5,3,10,1]{4,3,2,1,0:T(8,128)} collective-permute-done((f32[4,5,3,10,1]{4,3,2,1,0:T(8,128)}, f32[4,5,3,10,1]{4,3,2,1,0:T(8,128)}, u32[]{:S(2)}, u32[]{:S(2)}) %collective-permute-start.16) | collective-permute-done | bytes 2432 | tf_op jit(solution)/shard_map/ppermute | solution.py:16
  279.9 39.1 %all-reduce.1 = (f32[4,4]{0,1:T(4,128)S(1)}, f32[12,4]{0,1:T(4,128)S(1)}) all-reduce(f32[4,4]{0,1:T(4,128)S(1)} %convolution_bitcast_fusion.1, f32[12,4]{0,1:T(4,128)S(1)} %fusion), channel_id=1, replica_groups=mesh['gx'=2,'gy'=4,'gz'=4] {'gx','gy','gz'}, use_global_device_ids=true, to_apply=%region_8.10 | all-reduce | flops 64 | bytes 512 | tf_op jit(solution)/shard_map/psum | solution.py:97
  328.8 41.0 %subtract_divide_fusion.18 = (f32[1,4]{0,1:T(4,128)S(1)}, f32[1,4]{0,1:T(4,128)S(1)}, f32[1,4]{0,1:T(4,128)S(1)}, f32[1,4]{0,1:T(4,128)S(1)}, f32[1,4]{0,1:T(4,1...) fusion(f32[12,4]{0,1:T(4,128)S(1)} %fusion.30, ...), kind=kLoop, calls=%fused_computation.833 | loop fusion | flops 484 | bytes 600 | tf_op jit(solution)/shard_map/div | solution.py:35
  369.8 30.0 %subtract_divide_fusion.9 = (f32[1,4]{0,1:T(4,128)S(1)}, f32[1,4]{0,1:T(4,128)S(1)}, f32[1,4]{0,1:T(4,128)S(1)}, f32[1,4]{0,1:T(4,128)S(1)}, f32[1,4]{0,1:T(4,12...) fusion(f32[1,4]{0,1:T(4,128)S(1)} %get-tuple-element.27, ...), kind=kLoop, calls=%fused_computation.824 | loop fusion | flops 416 | bytes 532 | tf_op jit(solution)/shard_map/div | solution.py:46
  399.8 26.2 %subtract_divide_fusion.6 = f32[1,4]{0,1:T(4,128)S(1)} fusion(f32[1,4]{0,1:T(4,128)S(1)} %get-tuple-element.19, f32[1,4]{0,1:T(4,128)S(1)} %get-tuple-element.18, f32[1,4]{0,1:T(4,128)S(1)} %get-tuple-element.17, f32[1,4]{0,1:T(4,128)S(1)} %get-tuple-element.16, f32[1,4]{0,1:T(4,128)S(1)} %get-tuple-element.15, f32[1,4]{0,1:T(4,128)S(1)} %get-tuple-element.14, ...), kind=kLoop, calls=%fused_computation.821 | loop fusion | flops 324 | bytes 376 | tf_op jit(solution)/shard_map/div | solution.py:46
  426.1 18.9 %subtract_divide_fusion.7 = f32[1,4]{0,1:T(4,128)S(1)} fusion(f32[1,4]{0,1:T(4,128)S(1)} %get-tuple-element.19, f32[1,4]{0,1:T(4,128)S(1)} %get-tuple-element.18, f32[1,4]{0,1:T(4,128)S(1)} %get-tuple-element.17, f32[1,4]{0,1:T(4,128)S(1)} %get-tuple-element.16, f32[1,4]{0,1:T(4,128)S(1)} %get-tuple-element.15, f32[1,4]{0,1:T(4,128)S(1)} %get-tuple-element.14, ...), kind=kLoop, calls=%fused_computation.822 | loop fusion | flops 228 | bytes 312 | tf_op jit(solution)/shard_map/div | solution.py:46
  444.9 12.0 %subtract_divide_fusion.8 = f32[1,4]{0,1:T(4,128)S(1)} fusion(f32[1,4]{0,1:T(4,128)S(1)} %get-tuple-element.19, f32[1,4]{0,1:T(4,128)S(1)} %get-tuple-element.18, f32[1,4]{0,1:T(4,128)S(1)} %get-tuple-element.17, f32[1,4]{0,1:T(4,128)S(1)} %get-tuple-element.16, f32[1,4]{0,1:T(4,128)S(1)} %get-tuple-element.15, f32[1,4]{0,1:T(4,128)S(1)} %get-tuple-element.14, ...), kind=kLoop, calls=%fused_computation.823 | loop fusion | flops 144 | bytes 252 | tf_op jit(solution)/shard_map/div | solution.py:46
  470.0 11.6 %collective-permute-done.23 = f32[4,5,3,10,1]{4,3,2,1,0:T(8,128)S(1)} collective-permute-done((f32[4,5,3,10,1]{4,3,2,1,0:T(8,128)S(1)}, f32[4,5,3,10,1]{4,3,2,1,0:T(8,128)S(1)}, u32[]{:S(2)}, u32[]{:S(2)}) %collective-permute-start.23) | collective-permute-done | bytes 2432 | tf_op jit(solution)/shard_map/ppermute | solution.py:18
  481.5 9.8 %collective-permute-done.22 = f32[4,5,3,10,1]{4,3,2,1,0:T(8,128)S(1)} collective-permute-done((f32[4,5,3,10,1]{4,3,2,1,0:T(8,128)S(1)}, f32[4,5,3,10,1]{4,3,2,1,0:T(8,128)S(1)}, u32[]{:S(2)}, u32[]{:S(2)}) %collective-permute-start.22) | collective-permute-done | bytes 2432 | tf_op jit(solution)/shard_map/ppermute | solution.py:16
  493.4 2.8 bitcast_subtract_fusion
  (184 shorter events, 85.0 us)
Async XLA Ops:
  56.3 9.8 %collective-permute-start.1 = (f32[4,5,1,8,128]{4,3,2,1,0:T(8,128)S(1)}, f32[4,5,1,8,128]{4,3,2,1,0:T(8,128)S(1)}, u32[]{:S(2)}, u32[]{:S(2)}) collective-permute-start(f32[4,5,1,8,128]{4,3,2,1,0:T(8,128)S(1)} %pad_maximum_fusion.5), channel_id=1, source_target_pairs={{16,0},{0,16},{17,1},{1,17},{18,2},{2,18},{19,3},{3,19},{20,4},{4,... | collective-permute-start | bytes 245768 | tf_op jit(solution)/shard_map/ppermute | solution.py:18
  58.7 7.5 %collective-permute-start = (f32[4,5,1,8,128]{4,3,2,1,0:T(8,128)S(1)}, f32[4,5,1,8,128]{4,3,2,1,0:T(8,128)S(1)}, u32[]{:S(2)}, u32[]{:S(2)}) collective-permute-start(f32[4,5,1,8,128]{4,3,2,1,0:T(8,128)S(1)} %pad_maximum_fusion.5), channel_id=1, source_target_pairs={{0,16},{16,0},{1,17},{17,1},{2,18},{18,2},{3,19},{19,3},{4,20},{20... | collective-permute-start | bytes 245768 | tf_op jit(solution)/shard_map/ppermute | solution.py:16
  66.2 1.6 collective-permute-start.3
  66.2 3.8 collective-permute-start.2
  70.3 13.9 %collective-permute-start.5 = (f32[4,5,3,10,1]{4,3,2,1,0:T(8,128)S(1)}, f32[4,5,3,10,1]{4,3,2,1,0:T(8,128)S(1)}, u32[]{:S(2)}, u32[]{:S(2)}) collective-permute-start(f32[4,5,3,10,1]{4,3,2,1,0:T(8,128)S(1)} %get-tuple-element.618), channel_id=1, source_target_pairs={{1,0},{2,1},{3,2},{0,3},{5,4},{6,5},{7,6},{4,7},{9,8},{10,9},{11,1... | collective-permute-start | bytes 7208 | tf_op jit(solution)/shard_map/ppermute | solution.py:18
  72.5 23.3 %collective-permute-start.4 = (f32[4,5,3,10,1]{4,3,2,1,0:T(8,128)S(1)}, f32[4,5,3,10,1]{4,3,2,1,0:T(8,128)S(1)}, u32[]{:S(2)}, u32[]{:S(2)}) collective-permute-start(f32[4,5,3,10,1]{4,3,2,1,0:T(8,128)S(1)} %get-tuple-element.617), channel_id=1, source_target_pairs={{0,1},{1,2},{2,3},{3,0},{4,5},{5,6},{6,7},{7,4},{8,9},{9,10},{10,1... | collective-permute-start | bytes 7208 | tf_op jit(solution)/shard_map/ppermute | solution.py:16
  148.5 4.8 collective-permute-start.7
  150.8 4.4 collective-permute-start.6
  155.3 1.6 collective-permute-start.9
  155.4 3.4 collective-permute-start.8
  160.0 13.8 %collective-permute-start.11 = (f32[4,5,3,10,1]{4,3,2,1,0:T(8,128)}, f32[4,5,3,10,1]{4,3,2,1,0:T(8,128)}, u32[]{:S(2)}, u32[]{:S(2)}) collective-permute-start(f32[4,5,3,10,1]{4,3,2,1,0:T(8,128)} %get-tuple-element.616), channel_id=1, source_target_pairs={{1,0},{2,1},{3,2},{0,3},{5,4},{6,5},{7,6},{4,7},{9,8},{10,9},{11,1... | collective-permute-start | bytes 7208 | tf_op jit(solution)/shard_map/ppermute | solution.py:18
  161.9 22.5 %collective-permute-start.10 = (f32[4,5,3,10,1]{4,3,2,1,0:T(8,128)}, f32[4,5,3,10,1]{4,3,2,1,0:T(8,128)}, u32[]{:S(2)}, u32[]{:S(2)}) collective-permute-start(f32[4,5,3,10,1]{4,3,2,1,0:T(8,128)} %get-tuple-element.615), channel_id=1, source_target_pairs={{0,1},{1,2},{2,3},{3,0},{4,5},{5,6},{6,7},{7,4},{8,9},{9,10},{10,1... | collective-permute-start | bytes 7208 | tf_op jit(solution)/shard_map/ppermute | solution.py:16
  237.9 5.1 %collective-permute-start.13 = (f32[4,5,1,8,128]{4,3,2,1,0:T(8,128)S(1)}, f32[4,5,1,8,128]{4,3,2,1,0:T(8,128)S(1)}, u32[]{:S(2)}, u32[]{:S(2)}) collective-permute-start(f32[4,5,1,8,128]{4,3,2,1,0:T(8,128)S(1)} %pad_maximum_fusion.7), channel_id=1, source_target_pairs={{16,0},{0,16},{17,1},{1,17},{18,2},{2,18},{19,3},{3,19},{20,4},{4,... | collective-permute-start | bytes 245768 | tf_op jit(solution)/shard_map/ppermute | solution.py:18
  240.3 4.4 collective-permute-start.12
  244.8 1.6 collective-permute-start.15
  244.8 3.4 collective-permute-start.14
  249.4 14.2 %collective-permute-start.17 = (f32[4,5,3,10,1]{4,3,2,1,0:T(8,128)}, f32[4,5,3,10,1]{4,3,2,1,0:T(8,128)}, u32[]{:S(2)}, u32[]{:S(2)}) collective-permute-start(f32[4,5,3,10,1]{4,3,2,1,0:T(8,128)} %get-tuple-element.614), channel_id=1, source_target_pairs={{1,0},{2,1},{3,2},{0,3},{5,4},{6,5},{7,6},{4,7},{9,8},{10,9},{11,1... | collective-permute-start | bytes 7208 | tf_op jit(solution)/shard_map/ppermute | solution.py:18
  251.7 22.2 %collective-permute-start.16 = (f32[4,5,3,10,1]{4,3,2,1,0:T(8,128)}, f32[4,5,3,10,1]{4,3,2,1,0:T(8,128)}, u32[]{:S(2)}, u32[]{:S(2)}) collective-permute-start(f32[4,5,3,10,1]{4,3,2,1,0:T(8,128)} %get-tuple-element.613), channel_id=1, source_target_pairs={{0,1},{1,2},{2,3},{3,0},{4,5},{5,6},{6,7},{7,4},{8,9},{9,10},{10,1... | collective-permute-start | bytes 7208 | tf_op jit(solution)/shard_map/ppermute | solution.py:16
  457.3 4.9 collective-permute-start.19
  459.7 4.4 collective-permute-start.18
  464.2 1.6 collective-permute-start.21
  464.2 3.4 collective-permute-start.20
  467.9 13.6 %collective-permute-start.23 = (f32[4,5,3,10,1]{4,3,2,1,0:T(8,128)S(1)}, f32[4,5,3,10,1]{4,3,2,1,0:T(8,128)S(1)}, u32[]{:S(2)}, u32[]{:S(2)}) collective-permute-start(f32[4,5,3,10,1]{4,3,2,1,0:T(8,128)S(1)} %get-tuple-element.612), channel_id=1, source_target_pairs={{1,0},{2,1},{3,2},{0,3},{5,4},{6,5},{7,6},{4,7},{9,8},{10,9},{11,1... | collective-permute-start | bytes 7208 | tf_op jit(solution)/shard_map/ppermute | solution.py:18
  469.6 21.7 %collective-permute-start.22 = (f32[4,5,3,10,1]{4,3,2,1,0:T(8,128)S(1)}, f32[4,5,3,10,1]{4,3,2,1,0:T(8,128)S(1)}, u32[]{:S(2)}, u32[]{:S(2)}) collective-permute-start(f32[4,5,3,10,1]{4,3,2,1,0:T(8,128)S(1)} %get-tuple-element.611), channel_id=1, source_target_pairs={{0,1},{1,2},{2,3},{3,0},{4,5},{5,6},{6,7},{7,4},{8,9},{9,10},{10,1... | collective-permute-start | bytes 7208 | tf_op jit(solution)/shard_map/ppermute | solution.py:16
  (6 other events, 110.0 us)
where the time goes:
time: 499 us; the launch traced here: 496 us
  other arithmetic  182 us (36%)
  blocking collectives  158 us (32%)
  waiting for transfers between devices  114 us (23%)
  starting transfers between devices  20.5 us (4%)
  local copies, waits for them, and re-layouts  13.8 us (3%)
  matrix products  6.05 us (1%)
    psum x3, blocking collectives, shards(): lax.psum((dot_high(stacked, workspace.T), dot_high(workspace, workspace.T...  116 us
    div x4, other arithmetic, upper_solve(): solved[row_pos] = accum / factor[row_pos, row_pos]  87.1 us
    div x6, other arithmetic, lower_solve(): solved.append(accum / factor[row_pos, row_pos])  69.5 us
    ppermute x12, waiting for transfers between devices, extended(): lax.ppermute(head, axis, [((i + 1) % count, i) for i in range(count)])  58 us
    ppermute x12, waiting for transfers between devices, extended(): lax.ppermute(tail, axis, [(i, (i + 1) % count) for i in range(count)])  55.6 us
    psum x1, blocking collectives, shards(): start_matrix = lax.psum(dot_high(flat_rhs, flat_rhs.T), ('gx', 'gy', 'gz'))  41.9 us
    ppermute x12, starting transfers between devices, extended(): lax.ppermute(head, axis, [((i + 1) % count, i) for i in range(count)])  17.7 us
  transfers between devices with their start and end apart: 24, of which 22 were waited for; matrix products, arithmetic and copies ran while one was open for 2% of the time, Pallas kernels for 0%

commit v1 on v0

v1 whole, which is shorter than its diff:
```python
import functools

import jax
import jax.numpy as jnp
from jax import lax
from jax.experimental import pallas as pl
from jax.experimental.pallas import tpu as pltpu
from jax.sharding import PartitionSpec as P

STEPS = 3
CENTRE = 8.97
GROUP = 8
AXES = ("gx", "gy", "gz")

VMEM = pl.BlockSpec(memory_space=pltpu.VMEM)


def call(body, outs, operands, scratch=(), flops=100_000):
    moved = sum(o.size * 4 for o in outs) + sum(o.size * o.dtype.itemsize for o in operands)
    return pl.pallas_call(
        body,
        out_shape=outs,
        in_specs=[VMEM] * len(operands),
        out_specs=[VMEM] * len(outs),
        scratch_shapes=list(scratch),
        compiler_params=pltpu.CompilerParams(vmem_limit_bytes=24 * 1024 * 1024),
        cost_estimate=pl.CostEstimate(flops=flops, bytes_accessed=moved, transcendentals=0),
    )(*operands)


def shape(*dims):
    return jax.ShapeDtypeStruct(dims, jnp.float32)


def lane_ids(rows, lanes):
    return lax.broadcasted_iota(jnp.int32, (rows, lanes), 1)


def edge_tile(main, comp, rhs, comps, rows, lanes):
    lane = lane_ids(rows, lanes)
    place = lane % GROUP
    tile = jnp.zeros((rows, lanes), jnp.float32)
    for r in range(rhs):
        value = main(r * comps + comp)
        low = pltpu.roll(value, (r * GROUP + 3) % lanes, 1)
        high = pltpu.roll(value, (r * GROUP + 5) % lanes, 1)
        here = lane // GROUP == r
        tile = jnp.where(here & (place < 4), low, jnp.where(here, high, tile))
    return tile


def edges_kernel(rhs, comps, main_ref, edge_ref):
    _, rows, lanes = main_ref.shape
    for comp in range(comps):
        edge_ref[comp] = edge_tile(lambda i: main_ref[i], comp, rhs, comps, rows, lanes)


def blocks_kernel(layers, raw_ref, out_ref):
    def body(i, carry):
        own = raw_ref[9 + i].astype(jnp.float32)
        below = raw_ref[i].astype(jnp.float32)
        above = raw_ref[18 + i].astype(jnp.float32)
        out_ref[i] = own
        if layers == 2:
            out_ref[9 + i] = below + above
        else:
            out_ref[9 + i] = below
            out_ref[18 + i] = above
        return carry

    lax.fori_loop(0, 9, body, 0)


def assemble_kernel(rhs, comps, main_ref, edge_ref, first_ref, second_ref, out_ref):
    fields, rows, lanes = main_ref.shape
    even = lax.axis_index("gz") % 2 == 0
    place = lane_ids(rows, lanes) % GROUP
    for i in range(fields):
        out_ref[i] = main_ref[i]
    for comp in range(comps):
        one, two = first_ref[comp], second_ref[comp]
        above = jnp.where(even, one, two)
        below = jnp.where(even, two, one)
        ghost = jnp.where(place < 3, below, jnp.where(place > 4, above, edge_ref[comp]))
        out_ref[fields + comp] = ghost


def rows_kernel(layers, tiles, rows, *refs):
    ins, (first_ref, second_ref) = refs[:layers], refs[layers:]
    even = lax.axis_index("gy") % 2 == 0
    first_ref[...] = jnp.zeros_like(first_ref)
    second_ref[...] = jnp.zeros_like(second_ref)
    for layer in range(layers):
        head = ins[layer][pl.ds(0, tiles, stride=rows), :]
        tail = ins[layer][pl.ds(rows - 1, tiles, stride=rows), :]
        where = pl.ds(layer * tiles, tiles)
        first_ref[where, :] = jnp.where(even, tail, head)
        second_ref[where, :] = jnp.where(even, head, tail)


def operator_kernel(layers, rhs, comps, last, *refs):
    blocks_ref, first_ref, second_ref = refs[:3]
    field_refs = refs[3 : 3 + layers]
    fields = rhs * comps
    tiles, rows, lanes = field_refs[0].shape
    if last:
        early_refs = refs[3 + layers : -4]
        out_ref, gram_ref, moved_ref, pairs_ref = refs[-4:]
    else:
        product_ref, next_ref, edge_ref, moved_ref = refs[3 + layers :]

    even = lax.axis_index("gy") % 2 == 0
    sub = lax.broadcasted_iota(jnp.int32, (rows, lanes), 0)
    lane = lane_ids(rows, lanes)
    for layer in range(layers):
        for dy in range(3):
            def moved(tile):
                value = field_refs[layer][tile]
                if dy == 1:
                    return value
                at = layer * tiles + tile
                one = first_ref[pl.ds(at, 1), :]
                two = second_ref[pl.ds(at, 1), :]
                if dy == 2:
                    row = jnp.where(even, one, two)
                    return jnp.where(sub == rows - 1, row, pltpu.roll(value, rows - 1, 0))
                row = jnp.where(even, two, one)
                return jnp.where(sub == 0, row, pltpu.roll(value, 1, 0))

            for comp in range(comps):
                ghost = moved(fields + comp)
                for r in range(rhs):
                    tile = r * comps + comp
                    value = moved(tile)
                    at = layer * 9 + dy * 3
                    left = pltpu.roll(ghost, (-(r * GROUP + 2)) % lanes, 1)
                    right = pltpu.roll(ghost, (lanes - 1 - (r * GROUP + 5)) % lanes, 1)
                    moved_ref[at, tile] = jnp.where(lane == 0, left, pltpu.roll(value, 1, 1))
                    moved_ref[at + 1, tile] = value
                    moved_ref[at + 2, tile] = jnp.where(
                        lane == lanes - 1, right, pltpu.roll(value, lanes - 1, 1)
                    )

    def body(at, total):
        total = list(total)
        for source in range(comps):
            values = [moved_ref[at, r * comps + source] for r in range(rhs)]
            for comp in range(comps):
                block = blocks_ref[at, comp * comps + source]
                for r in range(rhs):
                    total[r * comps + comp] += block * values[r]
        return tuple(total)

    zero = jnp.zeros((rows, lanes), jnp.float32)
    total = lax.fori_loop(0, 9 * layers, body, (zero,) * fields)
    if not last:
        for i in range(fields):
            product_ref[i] = total[i]
            next_ref[i] = total[i] - CENTRE * field_refs[0][i]
        for comp in range(comps):
            edge_ref[comp] = edge_tile(lambda i: next_ref[i], comp, rhs, comps, rows, lanes)
        return
    for i in range(fields):
        out_ref[i] = total[i]
    start_ref, products = early_refs[0], list(early_refs[1:]) + [out_ref]
    for at, (one, two) in enumerate(gram_pairs(rhs)):
        left = products[one // rhs] if one >= 0 else start_ref
        first = (one % rhs if one >= 0 else -1 - one) * comps
        second = two % rhs * comps
        accum = None
        for comp in range(comps):
            term = left[first + comp] * products[two // rhs][second + comp]
            accum = term if accum is None else accum + term
        pairs_ref[pl.ds(at * rows, rows), :] = accum
    count = len(gram_pairs(rhs))
    for at in range(count, pairs_ref.shape[0] // rows):
        pairs_ref[pl.ds(at * rows, rows), :] = zero
    slots = pairs_ref.shape[0] // rows
    sums = pairs_ref[pl.ds(0, slots, stride=rows), :]
    for row in range(1, rows):
        sums = sums + pairs_ref[pl.ds(row, slots, stride=rows), :]
    sums = jnp.sum(sums, axis=1, keepdims=True)
    diagonal = lax.broadcasted_iota(jnp.int32, (slots, slots), 0) == lane_ids(slots, slots)
    packed = jnp.sum(jnp.where(diagonal, sums, 0.0), axis=0, keepdims=True)
    gram_ref[...] = jnp.broadcast_to(packed, gram_ref.shape)


def gram_pairs(rhs):
    size = rhs * STEPS
    pairs = [(i, j) for i in range(size) for j in range(i, size)]
    return pairs + [(-1 - r, j) for r in range(rhs) for j in range(size)]


def finish_kernel(rhs, comps, sums_ref, start_ref, *refs):
    basis = [start_ref, *refs[: STEPS - 1]]
    products = refs[STEPS - 1 : 2 * STEPS - 1]
    solution_ref, residual_ref = refs[2 * STEPS - 1 :]
    _, rows, lanes = start_ref.shape
    size = rhs * STEPS
    packed = jnp.sum(sums_ref[...], axis=0, keepdims=True)
    gram, right = {}, {}
    for at, (one, two) in enumerate(gram_pairs(rhs)):
        entry = jnp.broadcast_to(packed[:, at : at + 1], (rows, lanes))
        if one >= 0:
            gram[one, two] = entry
        else:
            right[two, -1 - one] = entry
    inverse = []
    for k in range(size):
        inverse.append(1.0 / gram[k, k])
        for i in range(k + 1, size):
            factor = gram[k, i] * inverse[k]
            for j in range(i, size):
                gram[i, j] = gram[i, j] - factor * gram[k, j]
            for r in range(rhs):
                right[i, r] = right[i, r] - factor * right[k, r]
    for r in range(rhs):
        weights = [None] * size
        for k in range(size - 1, -1, -1):
            accum = right[k, r]
            for j in range(k + 1, size):
                accum = accum - gram[k, j] * weights[j]
            weights[k] = accum * inverse[k]
        for comp in range(comps):
            answer = None
            image = None
            for k in range(size):
                tile = k % rhs * comps + comp
                one = weights[k] * basis[k // rhs][tile]
                two = weights[k] * products[k // rhs][tile]
                answer = one if answer is None else answer + one
                image = two if image is None else image + two
            solution_ref[r * comps + comp] = answer
            residual_ref[r * comps + comp] = start_ref[r * comps + comp] - image


def paired(count, ring):
    first = [(i, i ^ 1) for i in range(count)]
    second = []
    for i in range(1, count - 1, 2):
        second += [(i, i + 1), (i + 1, i)]
    if ring and count > 2:
        second += [(count - 1, 0), (0, count - 1)]
    return first, second


def swap(value, axis, pairs):
    return lax.ppermute(value, axis, pairs)


def shards(sizes, right_side, jacobian):
    rhs, comps, _, rows, lanes = right_side.shape
    fields, tiles = rhs * comps, (rhs + 1) * comps
    layers = 2 if sizes["gx"] == 2 else 3
    devices = sizes["gx"] * sizes["gy"] * sizes["gz"]
    start = right_side.reshape(fields, rows, lanes)
    raw = jacobian.reshape(27, comps * comps, rows, lanes)

    (blocks,) = call(
        functools.partial(blocks_kernel, layers), [shape(9 * layers, comps * comps, rows, lanes)], [raw]
    )
    (edge,) = call(functools.partial(edges_kernel, rhs, comps), [shape(comps, rows, lanes)], [start])

    z_pairs = paired(sizes["gz"], False)
    y_pairs = paired(sizes["gy"], True)
    packed_rows = -(-layers * tiles // 8) * 8
    slots = -(-len(gram_pairs(rhs)) // 8) * 8
    moved = pltpu.VMEM((9 * layers, fields, rows, lanes), jnp.float32)

    basis, products = [start], []
    for step in range(STEPS):
        below, above = (swap(edge, "gz", pairs) for pairs in z_pairs)
        (field,) = call(
            functools.partial(assemble_kernel, rhs, comps),
            [shape(tiles, rows, lanes)],
            [basis[-1], edge, below, above],
        )
        count = sizes["gx"]
        if layers == 2:
            slabs = [field, swap(field, "gx", [(0, 1), (1, 0)])]
        else:
            slabs = [
                field,
                swap(field, "gx", [(i, (i + 1) % count) for i in range(count)]),
                swap(field, "gx", [((i + 1) % count, i) for i in range(count)]),
            ]
        flat = [slab.reshape(tiles * rows, lanes) for slab in slabs]
        sent = call(
            functools.partial(rows_kernel, layers, tiles, rows),
            [shape(packed_rows, lanes)] * 2,
            flat,
        )
        first, second = (swap(value, "gy", pairs) for value, pairs in zip(sent, y_pairs))
        last = step == STEPS - 1
        flops = 2 * 9 * layers * comps * fields * rows * lanes
        if last:
            product, gram = call(
                functools.partial(operator_kernel, layers, rhs, comps, True),
                [shape(fields, rows, lanes), shape(devices, slots)],
                [blocks, first, second, *slabs, start, *products],
                [moved, pltpu.VMEM((slots * rows, lanes), jnp.float32)],
                flops,
            )
            products.append(product)
        else:
            product, following, edge = call(
                functools.partial(operator_kernel, layers, rhs, comps, False),
                [shape(fields, rows, lanes), shape(fields, rows, lanes), shape(comps, rows, lanes)],
                [blocks, first, second, *slabs],
                [moved],
                flops,
            )
            products.append(product)
            basis.append(following)

    sums = lax.all_to_all(gram, AXES, 0, 0, tiled=True)
    answer, residual = call(
        functools.partial(finish_kernel, rhs, comps),
        [shape(fields, rows, lanes)] * 2,
        [sums, *basis, *products],
    )
    return answer.reshape(right_side.shape), residual.reshape(right_side.shape)


def solution(mesh):
    cells = P(None, None, "gx", "gy", "gz")
    return jax.shard_map(
        functools.partial(shards, dict(mesh.shape)),
        mesh=mesh,
        in_specs=(cells, P(None, None, None, "gx", "gy", "gz")),
        out_specs=(cells, cells),
        check_vma=False,
    )
```

time: 499 us -> 65.4 us (0.13)
  other arithmetic: 182 us -> 0 us
  blocking collectives: 158 us -> 11.3 us
  waiting for transfers between devices: 114 us -> 18.5 us
  local copies, waits for them, and re-layouts: 13.8 us -> 2.23 us
  matrix products: 6.05 us -> 0 us
  starting transfers between devices: 20.5 us -> 26.5 us
  Pallas kernels: 0 us -> 5.78 us
    psum x4 -> x0, blocking collectives: 158 us -> none  [the longest x3 116 us: shards(): lax.psum((dot_high(stacked, workspace.T), dot_high(workspace, workspace.T...]
    div x15 -> x0, other arithmetic: 157 us -> none  [the longest x4 87.1 us: upper_solve(): solved[row_pos] = accum / factor[row_pos, row_pos]]
    ppermute x24 -> x15, waiting for transfers between devices: 114 us -> 18.5 us  [swap(): return lax.ppermute(value, axis, pairs)]
    all_to_all x0 -> x1, blocking collectives: none -> 11.3 us  [shards(): sums = lax.all_to_all(gram, AXES, 0, 0, tiled=True)]
    slice x12 -> x0, local copies, waits for them, and re-layouts: 8.19 us -> none  [the longest x4 2.61 us: extended(): lax.slice_in_dim(cells, cells.shape[dim] - width, cells.shape[dim], axis=...]
    add x3 -> x0, other arithmetic: 6.08 us -> none  [apply_operator(): total = total + block[None, :, source_comp] * piece[:, source_comp][:, None]]
    dot_general x15 -> x0, matrix products: 6.05 us -> none  [dot_high(): jnp.dot(left, right, precision=lax.Precision.HIGHEST, preferred_element_t...]
    ppermute x24 -> x15, starting transfers between devices: 20.5 us -> 26.5 us  [swap(): return lax.ppermute(value, axis, pairs)]
  transfers between devices with their start and end apart: 24 -> 15, of which waited for: 22 -> 9; matrix products, arithmetic and copies ran while one was open for 2% -> 0% of each run, Pallas kernels for 0% -> 0%
where the time goes in v1:
time: 65.4 us; the launch traced here: 65.1 us
  starting transfers between devices  26.5 us (41%)
  waiting for transfers between devices  18.5 us (28%)
  blocking collectives  11.3 us (17%)
  Pallas kernels  5.78 us (9%)
  local copies, waits for them, and re-layouts  2.23 us (3%)
  between operations  0.79 us (1%)
    ppermute x15, starting transfers between devices, swap(): return lax.ppermute(value, axis, pairs)  26.5 us
    ppermute x15, waiting for transfers between devices, swap(): return lax.ppermute(value, axis, pairs)  18.5 us
    all_to_all x1, blocking collectives, shards(): sums = lax.all_to_all(gram, AXES, 0, 0, tiled=True)  11.3 us
    pallas_call x12, Pallas kernels, call(): pl.pallas_call(body, out_shape=outs, in_specs=[VMEM] * len(operands), out...  5.78 us
    unnamed x6, local copies, waits for them, and re-layouts  2.23 us
  transfers between devices with their start and end apart: 15, of which 9 were waited for; matrix products, arithmetic and copies ran while one was open for 0% of the time, Pallas kernels for 0%

profile of v1, /device:TPU:0, one launch (start us, length us, event | category | flops | bytes accessed | tf_op | source)
XLA Modules:
  0.0 65.1 jit_solution(6532705917806314122)
XLA Ops:
  0.6 0.9 %copy-done.1 = f32[4,5,1,8,128]{4,3,2,1,0:T(8,128)S(1)} copy-done((f32[4,5,1,8,128]{4,3,2,1,0:T(8,128)S(1)}, f32[4,5,1,8,128]{4,3,2,1,0:T(8,128)}, u32[]{:S(2)}) %copy-start.1) | copy-done | bytes 81944
  2.3 5.9 %collective-permute-start = (f32[5,8,128]{2,1,0:T(8,128)S(1)}, f32[5,8,128]{2,1,0:T(8,128)S(1)}, u32[]{:S(2)}, u32[]{:S(2)}) collective-permute-start(f32[5,8,128]{2,1,0:T(8,128)S(1)} %shard_map.42.edge_ref), channel_id=1, source_target_pairs={{0,1},{1,0},{2,3},{3,2},{4,5},{5,4},{6,7},{7,6},{8,9},{9,8},{10,11... | collective-permute-start | bytes 61448 | tf_op jit(solution)/shard_map/ppermute | solution.py:248
  8.2 1.8 %collective-permute-done.first_ref = f32[5,8,128]{2,1,0:T(8,128)S(1)} collective-permute-done((f32[5,8,128]{2,1,0:T(8,128)S(1)}, f32[5,8,128]{2,1,0:T(8,128)S(1)}, u32[]{:S(2)}, u32[]{:S(2)}) %collective-permute-start) | collective-permute-done | bytes 20512 | tf_op jit(solution)/shard_map/ppermute | solution.py:248
  10.0 1.6 %collective-permute-start.2 = (f32[25,8,128]{2,1,0:T(8,128)S(1)}, f32[25,8,128]{2,1,0:T(8,128)S(1)}, u32[]{:S(2)}, u32[]{:S(2)}) collective-permute-start(f32[25,8,128]{2,1,0:T(8,128)S(1)} %shard_map.43.refs_3_), channel_id=1, source_target_pairs={{0,16},{16,0},{1,17},{17,1},{2,18},{18,2},{3,19},{19,3},{4,20},{20... | collective-permute-start | bytes 307208 | tf_op jit(solution)/shard_map/ppermute | solution.py:248
  11.6 3.2 %collective-permute-done.2.refs_4_ = f32[25,8,128]{2,1,0:T(8,128)S(1)} collective-permute-done((f32[25,8,128]{2,1,0:T(8,128)S(1)}, f32[25,8,128]{2,1,0:T(8,128)S(1)}, u32[]{:S(2)}, u32[]{:S(2)}) %collective-permute-start.2) | collective-permute-done | bytes 102432 | tf_op jit(solution)/shard_map/ppermute | solution.py:248
  14.9 1.6 %collective-permute-start.4 = (f32[56,128]{1,0:T(8,128)S(1)}, f32[56,128]{1,0:T(8,128)S(1)}, u32[]{:S(2)}, u32[]{:S(2)}) collective-permute-start(f32[56,128]{1,0:T(8,128)S(1)} %get-tuple-element.19), channel_id=1, source_target_pairs={{4,8},{8,4},{12,0},{0,12},{5,9},{9,5},{13,1},{1,13},{6,10},{10,6},... | collective-permute-start | bytes 86024 | tf_op jit(solution)/shard_map/ppermute | solution.py:248
  16.5 1.3 %copy-done = bf16[27,5,5,1,8,128]{5,4,3,2,1,0:T(8,128)(2,1)S(1)} copy-done((bf16[27,5,5,1,8,128]{5,4,3,2,1,0:T(8,128)(2,1)S(1)}, bf16[27,5,5,1,8,128]{5,4,3,2,1,0:T(8,128)(2,1)}, u32[]{:S(2)}) %copy-start) | copy-done | bytes 1382424
  18.2 1.3 %shard_map.45 = (f32[20,8,128]{2,1,0:T(8,128)S(1)}, f32[20,8,128]{2,1,0:T(8,128)S(1)}, f32[5,8,128]{2,1,0:T(8,128)S(1)}) custom-call(f32[18,25,8,128]{3,2,1,0:T(8,128)S(1)} %shard_map.41.refs_0_, f32[56,128]{1,0:T(8,128)S(1)} %collective-permute-done.3.refs_1_, f32[56,128]{1,0:T(8,128)S(1)} %collective-permute-done.4.refs_2_, ...), custom_call_target="tpu_custom_call" | custom-call | flops 3686400 | bytes 2289664 | tf_op jit(solution)/shard_map/pallas_call | solution.py:20
  20.4 3.8 %collective-permute-start.5 = (f32[5,8,128]{2,1,0:T(8,128)S(1)}, f32[5,8,128]{2,1,0:T(8,128)S(1)}, u32[]{:S(2)}, u32[]{:S(2)}) collective-permute-start(f32[5,8,128]{2,1,0:T(8,128)S(1)} %get-tuple-element.21.edge_ref), channel_id=1, source_target_pairs={{0,1},{1,0},{2,3},{3,2},{4,5},{5,4},{6,7},{7,6},{8,9},{9,8},{10,11... | collective-permute-start | bytes 61448 | tf_op jit(solution)/shard_map/ppermute | solution.py:248
  24.1 1.8 %collective-permute-done.5.first_ref = f32[5,8,128]{2,1,0:T(8,128)S(1)} collective-permute-done((f32[5,8,128]{2,1,0:T(8,128)S(1)}, f32[5,8,128]{2,1,0:T(8,128)S(1)}, u32[]{:S(2)}, u32[]{:S(2)}) %collective-permute-start.5) | collective-permute-done | bytes 20512 | tf_op jit(solution)/shard_map/ppermute | solution.py:248
  25.9 1.6 %collective-permute-start.7 = (f32[25,8,128]{2,1,0:T(8,128)S(1)}, f32[25,8,128]{2,1,0:T(8,128)S(1)}, u32[]{:S(2)}, u32[]{:S(2)}) collective-permute-start(f32[25,8,128]{2,1,0:T(8,128)S(1)} %shard_map.46.refs_3_), channel_id=1, source_target_pairs={{0,16},{16,0},{1,17},{17,1},{2,18},{18,2},{3,19},{19,3},{4,20},{20... | collective-permute-start | bytes 307208 | tf_op jit(solution)/shard_map/ppermute | solution.py:248
  27.5 3.2 %collective-permute-done.7.refs_4_ = f32[25,8,128]{2,1,0:T(8,128)S(1)} collective-permute-done((f32[25,8,128]{2,1,0:T(8,128)S(1)}, f32[25,8,128]{2,1,0:T(8,128)S(1)}, u32[]{:S(2)}, u32[]{:S(2)}) %collective-permute-start.7) | collective-permute-done | bytes 102432 | tf_op jit(solution)/shard_map/ppermute | solution.py:248
  30.8 1.6 %collective-permute-start.9 = (f32[56,128]{1,0:T(8,128)S(1)}, f32[56,128]{1,0:T(8,128)S(1)}, u32[]{:S(2)}, u32[]{:S(2)}) collective-permute-start(f32[56,128]{1,0:T(8,128)S(1)} %get-tuple-element.23), channel_id=1, source_target_pairs={{4,8},{8,4},{12,0},{0,12},{5,9},{9,5},{13,1},{1,13},{6,10},{10,6},... | collective-permute-start | bytes 86024 | tf_op jit(solution)/shard_map/ppermute | solution.py:248
  32.4 1.7 %collective-permute-done.9.refs_2_ = f32[56,128]{1,0:T(8,128)S(1)} collective-permute-done((f32[56,128]{1,0:T(8,128)S(1)}, f32[56,128]{1,0:T(8,128)S(1)}, u32[]{:S(2)}, u32[]{:S(2)}) %collective-permute-start.9) | collective-permute-done | bytes 28704 | tf_op jit(solution)/shard_map/ppermute | solution.py:248
  34.1 1.3 %shard_map.48 = (f32[20,8,128]{2,1,0:T(8,128)S(1)}, f32[20,8,128]{2,1,0:T(8,128)S(1)}, f32[5,8,128]{2,1,0:T(8,128)S(1)}) custom-call(f32[18,25,8,128]{3,2,1,0:T(8,128)S(1)} %shard_map.41.refs_0_, f32[56,128]{1,0:T(8,128)S(1)} %collective-permute-done.8.refs_1_, f32[56,128]{1,0:T(8,128)S(1)} %collective-permute-done.9.refs_2_, ...), custom_call_target="tpu_custom_call" | custom-call | flops 3686400 | bytes 2289664 | tf_op jit(solution)/shard_map/pallas_call | solution.py:20
  36.1 4.9 %collective-permute-start.10 = (f32[5,8,128]{2,1,0:T(8,128)S(1)}, f32[5,8,128]{2,1,0:T(8,128)S(1)}, u32[]{:S(2)}, u32[]{:S(2)}) collective-permute-start(f32[5,8,128]{2,1,0:T(8,128)S(1)} %get-tuple-element.25.edge_ref), channel_id=1, source_target_pairs={{0,1},{1,0},{2,3},{3,2},{4,5},{5,4},{6,7},{7,6},{8,9},{9,8},{10,11... | collective-permute-start | bytes 61448 | tf_op jit(solution)/shard_map/ppermute | solution.py:248
  41.0 1.8 %collective-permute-done.10.first_ref = f32[5,8,128]{2,1,0:T(8,128)S(1)} collective-permute-done((f32[5,8,128]{2,1,0:T(8,128)S(1)}, f32[5,8,128]{2,1,0:T(8,128)S(1)}, u32[]{:S(2)}, u32[]{:S(2)}) %collective-permute-start.10) | collective-permute-done | bytes 20512 | tf_op jit(solution)/shard_map/ppermute | solution.py:248
  42.8 1.6 %collective-permute-start.12 = (f32[25,8,128]{2,1,0:T(8,128)S(1)}, f32[25,8,128]{2,1,0:T(8,128)S(1)}, u32[]{:S(2)}, u32[]{:S(2)}) collective-permute-start(f32[25,8,128]{2,1,0:T(8,128)S(1)} %shard_map.49.refs_3_), channel_id=1, source_target_pairs={{0,16},{16,0},{1,17},{17,1},{2,18},{18,2},{3,19},{19,3},{4,20},{20... | collective-permute-start | bytes 307208 | tf_op jit(solution)/shard_map/ppermute | solution.py:248
  44.4 3.2 %collective-permute-done.12.refs_4_ = f32[25,8,128]{2,1,0:T(8,128)S(1)} collective-permute-done((f32[25,8,128]{2,1,0:T(8,128)S(1)}, f32[25,8,128]{2,1,0:T(8,128)S(1)}, u32[]{:S(2)}, u32[]{:S(2)}) %collective-permute-start.12) | collective-permute-done | bytes 102432 | tf_op jit(solution)/shard_map/ppermute | solution.py:248
  47.6 1.6 %collective-permute-start.14 = (f32[56,128]{1,0:T(8,128)S(1)}, f32[56,128]{1,0:T(8,128)S(1)}, u32[]{:S(2)}, u32[]{:S(2)}) collective-permute-start(f32[56,128]{1,0:T(8,128)S(1)} %get-tuple-element.27), channel_id=1, source_target_pairs={{4,8},{8,4},{12,0},{0,12},{5,9},{9,5},{13,1},{1,13},{6,10},{10,6},... | collective-permute-start | bytes 86024 | tf_op jit(solution)/shard_map/ppermute | solution.py:248
  49.3 1.7 %collective-permute-done.14.refs_2_ = f32[56,128]{1,0:T(8,128)S(1)} collective-permute-done((f32[56,128]{1,0:T(8,128)S(1)}, f32[56,128]{1,0:T(8,128)S(1)}, u32[]{:S(2)}, u32[]{:S(2)}) %collective-permute-start.14) | collective-permute-done | bytes 28704 | tf_op jit(solution)/shard_map/ppermute | solution.py:248
  51.0 1.5 %shard_map.51 = (f32[20,8,128]{2,1,0:T(8,128)S(1)}, f32[32,128]{1,0:T(8,128)S(1)}) custom-call(f32[18,25,8,128]{3,2,1,0:T(8,128)S(1)} %shard_map.41.refs_0_, f32[56,128]{1,0:T(8,128)S(1)} %collective-permute-done.13.refs_1_, f32[56,128]{1,0:T(8,128)S(1)} %collective-permute-done.14.refs_2_, f32[25,8,128]{2,1,0:T(8,128)S(1)} %shard_map.49.refs_3_, ...), custom_call_target="tpu_custom_call" | custom-call | flops 3686400 | bytes 2449408 | tf_op jit(solution)/shard_map/pallas_call | solution.py:20
  52.6 11.3 %all_to_all.11 = f32[32,1,128]{2,1,0:T(1,128)S(1)} all-to-all(f32[32,1,128]{2,1,0:T(1,128)S(1)} %bitcast.30), channel_id=1, replica_groups=mesh['gx'=2,'gy'=4,'gz'=4] {'gx','gy','gz'}, dimensions={0} | all-to-all | bytes 32768 | tf_op jit(solution)/shard_map/all_to_all | solution.py:316
  63.9 1.2 %shard_map.52 = (f32[20,8,128]{2,1,0:T(8,128)}, f32[20,8,128]{2,1,0:T(8,128)}) custom-call(f32[32,128]{1,0:T(8,128)S(1)} %bitcast.29, f32[20,8,128]{2,1,0:T(8,128)S(1)} %bitcast.22, f32[20,8,128]{2,1,0:T(8,128)S(1)} %get-tuple-element.20.main_ref.refs_0_, f32[20,8,128]{2,1,0:T(8,128)S(1)} %get-tuple-element.24.main_ref.refs_1_, ...), custom_call_target="tpu_custom_call" | custom-call | flops 100000 | bytes 671744 | tf_op jit(solution)/shard_map/pallas_call | solution.py:20
  (25 shorter events, 2.9 us)
Async XLA Ops:
  0.6 0.9 %copy-start.1 = (f32[4,5,1,8,128]{4,3,2,1,0:T(8,128)S(1)}, f32[4,5,1,8,128]{4,3,2,1,0:T(8,128)}, u32[]{:S(2)}) copy-start(f32[4,5,1,8,128]{4,3,2,1,0:T(8,128)} %param.2) | copy-start | bytes 245764
  1.6 6.6 %collective-permute-start.1 = (f32[5,8,128]{2,1,0:T(8,128)S(1)}, f32[5,8,128]{2,1,0:T(8,128)S(1)}, u32[]{:S(2)}, u32[]{:S(2)}) collective-permute-start(f32[5,8,128]{2,1,0:T(8,128)S(1)} %shard_map.42.edge_ref), channel_id=1, source_target_pairs={{1,2},{2,1},{5,6},{6,5},{9,10},{10,9},{13,14},{14,13},{17,18},{18,... | collective-permute-start | bytes 61448 | tf_op jit(solution)/shard_map/ppermute | solution.py:248
  2.3 7.7 %collective-permute-start = (f32[5,8,128]{2,1,0:T(8,128)S(1)}, f32[5,8,128]{2,1,0:T(8,128)S(1)}, u32[]{:S(2)}, u32[]{:S(2)}) collective-permute-start(f32[5,8,128]{2,1,0:T(8,128)S(1)} %shard_map.42.edge_ref), channel_id=1, source_target_pairs={{0,1},{1,0},{2,3},{3,2},{4,5},{5,4},{6,7},{7,6},{8,9},{9,8},{10,11... | collective-permute-start | bytes 61448 | tf_op jit(solution)/shard_map/ppermute | solution.py:248
  10.0 4.7 %collective-permute-start.2 = (f32[25,8,128]{2,1,0:T(8,128)S(1)}, f32[25,8,128]{2,1,0:T(8,128)S(1)}, u32[]{:S(2)}, u32[]{:S(2)}) collective-permute-start(f32[25,8,128]{2,1,0:T(8,128)S(1)} %shard_map.43.refs_3_), channel_id=1, source_target_pairs={{0,16},{16,0},{1,17},{17,1},{2,18},{18,2},{3,19},{19,3},{4,20},{20... | collective-permute-start | bytes 307208 | tf_op jit(solution)/shard_map/ppermute | solution.py:248
  14.8 3.2 %collective-permute-start.3 = (f32[56,128]{1,0:T(8,128)S(1)}, f32[56,128]{1,0:T(8,128)S(1)}, u32[]{:S(2)}, u32[]{:S(2)}) collective-permute-start(f32[56,128]{1,0:T(8,128)S(1)} %get-tuple-element.18), channel_id=1, source_target_pairs={{0,4},{4,0},{8,12},{12,8},{1,5},{5,1},{9,13},{13,9},{2,6},{6,2},{1... | collective-permute-start | bytes 86024 | tf_op jit(solution)/shard_map/ppermute | solution.py:248
  14.9 3.4 %collective-permute-start.4 = (f32[56,128]{1,0:T(8,128)S(1)}, f32[56,128]{1,0:T(8,128)S(1)}, u32[]{:S(2)}, u32[]{:S(2)}) collective-permute-start(f32[56,128]{1,0:T(8,128)S(1)} %get-tuple-element.19), channel_id=1, source_target_pairs={{4,8},{8,4},{12,0},{0,12},{5,9},{9,5},{13,1},{1,13},{6,10},{10,6},... | collective-permute-start | bytes 86024 | tf_op jit(solution)/shard_map/ppermute | solution.py:248
  16.5 1.3 %copy-start = (bf16[27,5,5,1,8,128]{5,4,3,2,1,0:T(8,128)(2,1)S(1)}, bf16[27,5,5,1,8,128]{5,4,3,2,1,0:T(8,128)(2,1)}, u32[]{:S(2)}) copy-start(bf16[27,5,5,1,8,128]{5,4,3,2,1,0:T(8,128)(2,1)} %param.3) | copy-start | bytes 4147204
  19.5 31.5 %copy-start.2 = (f32[4,5,1,8,128]{4,3,2,1,0:T(8,128)S(1)}, f32[4,5,1,8,128]{4,3,2,1,0:T(8,128)}, u32[]{:S(2)}) copy-start(f32[4,5,1,8,128]{4,3,2,1,0:T(8,128)} %param.2) | copy-start | bytes 245764
  19.6 4.6 %collective-permute-start.6 = (f32[5,8,128]{2,1,0:T(8,128)S(1)}, f32[5,8,128]{2,1,0:T(8,128)S(1)}, u32[]{:S(2)}, u32[]{:S(2)}) collective-permute-start(f32[5,8,128]{2,1,0:T(8,128)S(1)} %get-tuple-element.21.edge_ref), channel_id=1, source_target_pairs={{1,2},{2,1},{5,6},{6,5},{9,10},{10,9},{13,14},{14,13},{17,18},{18,... | collective-permute-start | bytes 61448 | tf_op jit(solution)/shard_map/ppermute | solution.py:248
  20.4 5.5 %collective-permute-start.5 = (f32[5,8,128]{2,1,0:T(8,128)S(1)}, f32[5,8,128]{2,1,0:T(8,128)S(1)}, u32[]{:S(2)}, u32[]{:S(2)}) collective-permute-start(f32[5,8,128]{2,1,0:T(8,128)S(1)} %get-tuple-element.21.edge_ref), channel_id=1, source_target_pairs={{0,1},{1,0},{2,3},{3,2},{4,5},{5,4},{6,7},{7,6},{8,9},{9,8},{10,11... | collective-permute-start | bytes 61448 | tf_op jit(solution)/shard_map/ppermute | solution.py:248
  25.9 4.7 %collective-permute-start.7 = (f32[25,8,128]{2,1,0:T(8,128)S(1)}, f32[25,8,128]{2,1,0:T(8,128)S(1)}, u32[]{:S(2)}, u32[]{:S(2)}) collective-permute-start(f32[25,8,128]{2,1,0:T(8,128)S(1)} %shard_map.46.refs_3_), channel_id=1, source_target_pairs={{0,16},{16,0},{1,17},{17,1},{2,18},{18,2},{3,19},{19,3},{4,20},{20... | collective-permute-start | bytes 307208 | tf_op jit(solution)/shard_map/ppermute | solution.py:248
  30.7 1.7 %collective-permute-start.8 = (f32[56,128]{1,0:T(8,128)S(1)}, f32[56,128]{1,0:T(8,128)S(1)}, u32[]{:S(2)}, u32[]{:S(2)}) collective-permute-start(f32[56,128]{1,0:T(8,128)S(1)} %get-tuple-element.22), channel_id=1, source_target_pairs={{0,4},{4,0},{8,12},{12,8},{1,5},{5,1},{9,13},{13,9},{2,6},{6,2},{1... | collective-permute-start | bytes 86024 | tf_op jit(solution)/shard_map/ppermute | solution.py:248
  30.8 3.4 %collective-permute-start.9 = (f32[56,128]{1,0:T(8,128)S(1)}, f32[56,128]{1,0:T(8,128)S(1)}, u32[]{:S(2)}, u32[]{:S(2)}) collective-permute-start(f32[56,128]{1,0:T(8,128)S(1)} %get-tuple-element.23), channel_id=1, source_target_pairs={{4,8},{8,4},{12,0},{0,12},{5,9},{9,5},{13,1},{1,13},{6,10},{10,6},... | collective-permute-start | bytes 86024 | tf_op jit(solution)/shard_map/ppermute | solution.py:248
  35.5 5.6 %collective-permute-start.11 = (f32[5,8,128]{2,1,0:T(8,128)S(1)}, f32[5,8,128]{2,1,0:T(8,128)S(1)}, u32[]{:S(2)}, u32[]{:S(2)}) collective-permute-start(f32[5,8,128]{2,1,0:T(8,128)S(1)} %get-tuple-element.25.edge_ref), channel_id=1, source_target_pairs={{1,2},{2,1},{5,6},{6,5},{9,10},{10,9},{13,14},{14,13},{17,18},{18,... | collective-permute-start | bytes 61448 | tf_op jit(solution)/shard_map/ppermute | solution.py:248
  36.1 6.7 %collective-permute-start.10 = (f32[5,8,128]{2,1,0:T(8,128)S(1)}, f32[5,8,128]{2,1,0:T(8,128)S(1)}, u32[]{:S(2)}, u32[]{:S(2)}) collective-permute-start(f32[5,8,128]{2,1,0:T(8,128)S(1)} %get-tuple-element.25.edge_ref), channel_id=1, source_target_pairs={{0,1},{1,0},{2,3},{3,2},{4,5},{5,4},{6,7},{7,6},{8,9},{9,8},{10,11... | collective-permute-start | bytes 61448 | tf_op jit(solution)/shard_map/ppermute | solution.py:248
  42.8 4.7 %collective-permute-start.12 = (f32[25,8,128]{2,1,0:T(8,128)S(1)}, f32[25,8,128]{2,1,0:T(8,128)S(1)}, u32[]{:S(2)}, u32[]{:S(2)}) collective-permute-start(f32[25,8,128]{2,1,0:T(8,128)S(1)} %shard_map.49.refs_3_), channel_id=1, source_target_pairs={{0,16},{16,0},{1,17},{17,1},{2,18},{18,2},{3,19},{19,3},{4,20},{20... | collective-permute-start | bytes 307208 | tf_op jit(solution)/shard_map/ppermute | solution.py:248
  47.6 1.7 %collective-permute-start.13 = (f32[56,128]{1,0:T(8,128)S(1)}, f32[56,128]{1,0:T(8,128)S(1)}, u32[]{:S(2)}, u32[]{:S(2)}) collective-permute-start(f32[56,128]{1,0:T(8,128)S(1)} %get-tuple-element.26), channel_id=1, source_target_pairs={{0,4},{4,0},{8,12},{12,8},{1,5},{5,1},{9,13},{13,9},{2,6},{6,2},{1... | collective-permute-start | bytes 86024 | tf_op jit(solution)/shard_map/ppermute | solution.py:248
  47.6 3.4 %collective-permute-start.14 = (f32[56,128]{1,0:T(8,128)S(1)}, f32[56,128]{1,0:T(8,128)S(1)}, u32[]{:S(2)}, u32[]{:S(2)}) collective-permute-start(f32[56,128]{1,0:T(8,128)S(1)} %get-tuple-element.27), channel_id=1, source_target_pairs={{4,8},{8,4},{12,0},{0,12},{5,9},{9,5},{13,1},{1,13},{6,10},{10,6},... | collective-permute-start | bytes 86024 | tf_op jit(solution)/shard_map/ppermute | solution.py:248
